TPU v7x, 32 devices: a whole 2x2x4 slice. The times are simulated.
32 devices in a mesh: seq: 2 (over x), expert: 16 (over z, y, core).
Axes of the slice: x: 2, y: 2, z: 4, core: 2. Of those that a mesh axis runs over, the one named last changes fastest.
Arguments:
- tokens: bfloat16 [768, 7168], P('expert', 'seq'), may hold values from -6 to 6
- expert_ids: int32 [768, 8], P('expert'), may hold values from 0 to 15, all different within a row
- route_weights: float32 [768, 8], P('expert'), may hold values from 0.05 to 1
- capacity: int32 [16], replicated, may hold values from 6 to 12
- expert_gate_up: bfloat16 [16, 2, 1024, 7168], P('expert', None, 'seq'), may hold values from -0.0625 to 0.0625
- expert_down: bfloat16 [16, 1024, 7168], P('expert', None, 'seq'), may hold values from -0.1875 to 0.1875
Outputs:
- mixed: bfloat16 [768, 7168], P('expert', 'seq')
Inputs may be any that keep to these rules, and one draw needn't show every extreme that they name: `expert_ids`: each row names 8 different experts.
All inputs are finite; a program needn't handle non-finite values.
Results may differ from a plain program's by a relative error of at most 0.02.
Values may be sent and summed in bfloat16 or wider, within the bound.
A program may use at most 128 MiB of HBM per device.

v0:
```python
import jax
import jax.numpy as jnp
from jax import lax
from jax.sharding import PartitionSpec as P

CAP = 12


def body(tokens, expert_ids, route_weights, capacity, expert_gate_up, expert_down):
    row_count = tokens.shape[0]
    share = tokens.shape[1]
    top_count = expert_ids.shape[1]
    expert_count = capacity.shape[0]
    slot_count = expert_count * CAP
    flat_ids = expert_ids.reshape(-1)
    one_hot = (flat_ids[:, None] == jnp.arange(expert_count, dtype=jnp.int32)[None, :]).astype(
        jnp.int32
    )
    within = jnp.sum((jnp.cumsum(one_hot, axis=0) - one_hot) * one_hot, axis=1)
    retained = within < jnp.sum(one_hot * capacity[None, :], axis=1)
    slot_of = flat_ids * CAP + within
    matches = jnp.logical_and(
        slot_of[None, :] == jnp.arange(slot_count, dtype=jnp.int32)[:, None], retained[None, :]
    )
    match_float = matches.astype(jnp.float32)
    weight_flat = route_weights.reshape(-1)
    mixing = jnp.sum(
        (match_float * weight_flat[None, :]).reshape(slot_count, row_count, top_count), axis=2
    )
    placing = jnp.sum(match_float.reshape(slot_count, row_count, top_count), axis=2).astype(
        jnp.bfloat16
    )
    buffer = jnp.dot(placing, tokens, preferred_element_type=jnp.float32).astype(jnp.bfloat16)
    received = lax.all_to_all(
        buffer.reshape(expert_count, CAP, share), "expert", split_axis=0, concat_axis=0, tiled=True
    )
    rows = received.reshape(slot_count, share)
    weights = expert_gate_up[0]
    hidden_share = weights.shape[1]
    piece = lax.all_gather(rows, "seq", axis=1, tiled=True)
    blocks = piece.shape[1] // share
    piece_blocks = piece.reshape(slot_count, blocks, share)
    column_blocks = weights.reshape(2, hidden_share, blocks, share)
    partial_value = jnp.einsum(
        "rks,gfks->krgf", piece_blocks, column_blocks, preferred_element_type=jnp.float32
    )
    rounded = lax.optimization_barrier(partial_value.astype(jnp.bfloat16))
    gate_up = jnp.sum(rounded.astype(jnp.float32), axis=0)
    hidden = (jax.nn.silu(gate_up[:, 0]) * gate_up[:, 1]).astype(jnp.bfloat16)
    down = expert_down[0]
    outputs = jnp.dot(
        lax.all_gather(hidden, "seq", axis=1, tiled=True), down, preferred_element_type=jnp.float32
    )
    outputs = outputs.astype(jnp.bfloat16).reshape(expert_count, CAP, share)
    back = lax.all_to_all(outputs, "expert", split_axis=0, concat_axis=0, tiled=True)
    mixed = jnp.dot(
        mixing.T,
        back.reshape(slot_count, share).astype(jnp.float32),
        precision=lax.Precision.HIGHEST,
    )
    return mixed.astype(jnp.bfloat16)


def solution(mesh):
    in_specs = (
        P("expert", "seq"),
        P("expert", None),
        P("expert", None),
        P(),
        P("expert", None, "seq", None),
        P("expert", None, "seq"),
    )
    out_specs = P("expert", "seq")
    return jax.shard_map(body, mesh=mesh, in_specs=in_specs, out_specs=out_specs, check_vma=False)
```

profile of v0, /device:TPU:0, one launch (start us, length us, event | category | flops | bytes accessed | tf_op | source)
XLA Modules:
  0.0 196.6 jit_solution(2475314111712754344)
XLA Ops:
  6.5 0.0 copy-start
  6.5 0.0 all-gather.2.cloned.1.call-start
  6.5 0.8 copy.37
  7.4 0.1 eq.44
  7.4 0.1 eq.40
  7.5 0.9 reduce-window.6
  8.4 0.2 slice_reduce_fusion
  8.7 0.8 select_reduce_fusion.1
  9.4 0.1 reduce_sum.52
  9.5 0.1 reduce_sum.50
  9.6 0.1 copy.40
  9.7 0.7 multiply_add_fusion
  10.4 0.1 copy.41
  10.5 0.8 copy.42
  11.2 1.0 convert_reduce_fusion.1
  12.2 0.0 copy-done
  12.2 0.5 convolution_convert_fusion
  12.7 0.4 reshape.84
  13.1 49.9 %all_to_all.10 = bf16[16,12,3584]{2,1,0:T(8,128)(2,1)} all-to-all(bf16[16,12,3584]{2,1,0:T(8,128)(2,1)S(1)} %reshape.84), channel_id=1, replica_groups=mesh['seq'=2,'expert'=16] {'expert'}, dimensions={0} | all-to-all | bytes 2752512 | tf_op jit(solution)/shard_map/all_to_all | solution.py:34
  63.0 3.4 %reshape.85 = bf16[192,3584]{1,0:T(8,128)(2,1)} reshape(bf16[16,12,3584]{2,1,0:T(8,128)(2,1)} %all_to_all.10) | data formatting | bytes 2752512 | tf_op jit(solution)/shard_map/reshape | solution.py:37
  66.4 0.0 all-gather.2.cloned.1.call-update
  66.5 32.1 %reshape_squeeze.3 = bf16[2,512,2,3584]{3,2,1,0:T(2,128)(2,1)} reshape(bf16[1,2,512,7168]{3,2,1,0:T(8,128)(2,1)} %param.10) | data formatting | bytes 29360128 | tf_op jit(solution)/shard_map/reshape;squeeze | solution.py:43
  98.6 7.9 %all-gather.2.cloned.1.call-done = bf16[192,7168]{1,0:T(8,128)(2,1)} async-done(((bf16[192,3584]{1,0:T(8,128)(2,1)}), bf16[192,7168]{1,0:T(8,128)(2,1)}) %all-gather.2.cloned.1.call-update) | async-done | bytes 2752528 | tf_op jit(solution)/shard_map/all_gather | solution.py:40
  106.5 6.3 %reshape.86 = bf16[192,2,3584]{2,1,0:T(2,128)(2,1)S(1)} reshape(bf16[192,7168]{1,0:T(8,128)(2,1)} %all-gather.2.cloned.1.call-done) | data formatting | bytes 5505024 | tf_op jit(solution)/shard_map/reshape | solution.py:42
  112.8 11.0 %fusion.8 = bf16[2,192,2,512]{3,1,2,0:T(8,128)(2,1)} fusion(bf16[2,512,2,3584]{3,2,1,0:T(2,128)(2,1)} %reshape_squeeze.3, bf16[192,2,3584,1]{2,1,0,3:T(2,128)(2,1)S(1)} %bitcast.43), kind=kOutput, calls=%fused_computation.9 | convolution fusion | flops 2818965504 | bytes 18219008 | tf_op jit(solution)/shard_map/rks,gfks->krgf/dot_general | solution.py:44
  123.8 1.3 convert_reduce_fusion
  125.2 0.1 fusion.14
  125.3 7.1 %all_gather.7 = bf16[192,1024]{1,0:T(8,128)(2,1)S(1)} all-gather(bf16[192,512]{1,0:T(8,128)(2,1)S(1)} %fusion.14), channel_id=1, replica_groups=mesh['seq'=2,'expert'=16] {'seq'}, dimensions={1}, use_global_device_ids=true | all-gather | bytes 589824 | tf_op jit(solution)/shard_map/all_gather | solution.py:52
  132.4 4.7 %fusion.4 = bf16[192,3584]{1,0:T(8,128)(2,1)S(1)} fusion(bf16[192,1024]{1,0:T(8,128)(2,1)S(1)} %all_gather.7, bf16[1,1024,3584]{2,1,0:T(8,128)(2,1)} %param.11), kind=kOutput, calls=%fused_computation.4 | convolution fusion | flops 1409974272 | bytes 9109504 | tf_op jit(solution)/shard_map/dot_general | solution.py:51
  137.2 0.4 reshape.87
  137.5 0.0 copy-start.1
  137.5 48.2 %all_to_all.11 = bf16[16,12,3584]{2,1,0:T(8,128)(2,1)} all-to-all(bf16[16,12,3584]{2,1,0:T(8,128)(2,1)S(1)} %reshape.87), channel_id=1, replica_groups=mesh['seq'=2,'expert'=16] {'expert'}, dimensions={0} | all-to-all | bytes 2752512 | tf_op jit(solution)/shard_map/all_to_all | solution.py:55
  185.8 2.4 %reshape.88 = bf16[192,3584]{1,0:T(8,128)(2,1)S(1)} reshape(bf16[16,12,3584]{2,1,0:T(8,128)(2,1)} %all_to_all.11) | data formatting | bytes 2752512 | tf_op jit(solution)/shard_map/reshape | solution.py:58
  188.2 0.0 copy-done.1
  188.2 1.6 convolution_convert_fusion.1
  (3 shorter events, 0.1 us)
Async XLA Ops:
  6.5 5.7 %copy-start = (bf16[48,3584]{1,0:T(8,128)(2,1)S(1)}, bf16[48,3584]{1,0:T(8,128)(2,1)}, u32[]{:S(2)}) copy-start(bf16[48,3584]{1,0:T(8,128)(2,1)} %param.6) | copy-start | bytes 1032196
  6.5 100.0 %all-gather.2.cloned.1.call-start = ((), (), s32[]{:S(2)}) async-start(), calls=%async_computation.2 | async-start | bytes 4128768 | tf_op jit(solution)/shard_map/all_gather | solution.py:40
  137.5 50.6 %copy-start.1 = (f32[192,48]{0,1:T(8,128)S(1)}, f32[192,48]{0,1:T(8,128)}, u32[]{:S(2)}) copy-start(f32[192,48]{0,1:T(8,128)} %get-tuple-element.6) | copy-start | bytes 110596
Sparse Core Ops, SparseCore 0:
  66.6 39.8 all-gather.1
where the time goes:
time: 198 us; the launch traced here: 197 us
  blocking collectives  105 us (53%)
  local copies, waits for them, and re-layouts  47.2 us (24%)
  matrix products  17.8 us (9%)
  between operations  13.5 us (7%)
  waiting for transfers between devices  7.89 us (4%)
  other arithmetic  4.79 us (2%)
    all_to_all x1, blocking collectives, body(): lax.all_to_all(buffer.reshape(expert_count, CAP, share), 'expert', split_...  49.9 us
    all_to_all x1, blocking collectives, body(): lax.all_to_all(outputs, 'expert', split_axis=0, concat_axis=0, tiled=True)  48.2 us
    another operation x1, local copies, waits for them, and re-layouts, body(): column_blocks = weights.reshape(2, hidden_share, blocks, share)  32.1 us
    dot_general x1, matrix products, body(): jnp.einsum('rks,gfks->krgf', piece_blocks, column_blocks, preferred_eleme...  11 us
    all_gather x1, waiting for transfers between devices, body(): piece = lax.all_gather(rows, 'seq', axis=1, tiled=True)  7.88 us
    all_gather x1, blocking collectives, body(): lax.all_gather(hidden, 'seq', axis=1, tiled=True)  7.14 us
    reshape x1, local copies, waits for them, and re-layouts, body(): piece_blocks = piece.reshape(slot_count, blocks, share)  6.29 us
    dot_general x1, matrix products, body(): jnp.dot(lax.all_gather(hidden, 'seq', axis=1, tiled=True), down, preferre...  4.71 us
  transfers between devices with their start and end apart: 1, of which 1 were waited for; matrix products, arithmetic and copies ran while one was open for 16% of the time, Pallas kernels for 0%

commit v1 on v0

v1 whole, which is shorter than its diff:
```python
import functools

import jax
import jax.numpy as jnp
from jax import lax
from jax.experimental import pallas as pl
from jax.experimental.pallas import tpu as pltpu
from jax.sharding import PartitionSpec as P

CAP = 12
MESH = pl.DeviceIdType.MESH
F32 = jnp.float32
BF16 = jnp.bfloat16


def kernel(
    n_seq, n_expert, info_ref, tokens_ref, gate_up_ref, down_ref, out_ref,
    wgu, wdn, tok, info, xr, hb, mine, pout, dd, sr, sl, rr, ll,
    local_sem, info_s, info_r, ag_s, ag_r, tw_s, tw_r, x_s, x_r, h_s, h_r, p_s, p_r, rs_s, rs_r,
):
    chips = n_expert // 2
    far = chips // 2
    group, half = tok.shape[3], tok.shape[4]
    share = 2 * half
    hid = wgu.shape[1]
    me_e = lax.axis_index("expert")
    me_s = lax.axis_index("seq")
    core = lax.rem(me_e, 2)
    chip = lax.div(me_e, 2)
    odd = lax.rem(chip, 2)
    pos = (1 - odd) * lax.div(chip, 2) + odd * (chips - 1 - lax.div(chip, 2))

    def device_at(offset, same_core):
        at = lax.rem(pos + offset + 2 * chips, chips)
        back = lax.div(at, far)
        there = (1 - back) * 2 * at + back * (2 * (chips - 1 - at) + 1)
        return there * 2 + (core if same_core else 1 - core)

    right, left, twin = device_at(1, True), device_at(-1, True), device_at(0, False)

    def remote(src, dst, send, recv, device):
        return pltpu.make_async_remote_copy(
            src_ref=src, dst_ref=dst, send_sem=send, recv_sem=recv,
            device_id=device, device_id_type=MESH,
        )

    def info_copy(d, cr):
        to = device_at(-d, cr == 0)
        return remote(info_ref.at[to], info.at[d, cr], info_s.at[d, cr], info_r.at[d, cr], {"expert": to})

    def gather_copy(way, k, h):
        src = lax.rem(chips - k + 1, chips) if way == 0 else k - 1
        dst = chips - k if way == 0 else k
        return remote(
            tok.at[src, 0, h], tok.at[dst, 0, h], ag_s.at[way, k - 1, h], ag_r.at[way, k - 1, h],
            {"expert": right if way == 0 else left},
        )

    def twin_copy(d, h):
        return remote(tok.at[d, 0, h], tok.at[d, 1, h], tw_s.at[d, h], tw_r.at[d, h], {"expert": twin})

    def rows_copy(k, o, receive=False):
        slot = lax.rem(me_s - o + n_seq, n_seq) if receive else me_s
        return remote(
            xr.at[k - 1, slot], xr.at[k - 1, slot], x_s.at[k - 1, o - 1], x_r.at[k - 1, o - 1],
            {"seq": lax.rem(me_s + o, n_seq)},
        )

    def hidden_copy(k, o, receive=False):
        slot = lax.rem(me_s - o + n_seq, n_seq) if receive else me_s
        return remote(
            hb.at[k - 1, slot], hb.at[k - 1, slot], h_s.at[k - 1, o - 1], h_r.at[k - 1, o - 1],
            {"seq": lax.rem(me_s + o, n_seq)},
        )

    def partial_copy(d, h):
        return remote(pout.at[d, h], dd.at[d, h], p_s.at[d, h], p_r.at[d, h], {"expert": twin})

    def sum_copy(way, k, h):
        src, dst = (sr, rr) if way == 0 else (sl, ll)
        return remote(
            src.at[k - 1, h], dst.at[k - 1, h], rs_s.at[way, k - 1, h], rs_r.at[way, k - 1, h],
            {"expert": right if way == 0 else left},
        )

    load_tokens = pltpu.make_async_copy(tokens_ref, tok.at[0, 0], local_sem.at[0])
    load_info = pltpu.make_async_copy(info_ref.at[me_e], info.at[0, 0], local_sem.at[1])
    load_gu = pltpu.make_async_copy(gate_up_ref, wgu, local_sem.at[2])
    load_dn = pltpu.make_async_copy(down_ref, wdn, local_sem.at[3])
    load_tokens.start()
    load_info.start()
    load_gu.start()
    load_dn.start()

    barrier = pltpu.get_barrier_semaphore()
    for o in range(1, n_expert):
        pl.semaphore_signal(
            barrier, inc=1, device_id={"expert": lax.rem(me_e + o, n_expert)}, device_id_type=MESH
        )
    for o in range(1, n_seq):
        pl.semaphore_signal(
            barrier, inc=1, device_id={"seq": lax.rem(me_s + o, n_seq)}, device_id_type=MESH
        )
    load_tokens.wait()
    load_info.wait()
    pl.semaphore_wait(barrier, n_expert - 1 + n_seq - 1)

    others = [(d, cr) for d in range(chips) for cr in range(2) if d or cr]
    for way, h in ((0, 0), (1, 1), (0, 1), (1, 0)):
        gather_copy(way, 1, h).start()
    for h in range(2):
        twin_copy(0, h).start()
    for d, cr in others:
        info_copy(d, cr).start()

    def pair(k):
        return k, (chips - k) * (1 - lax.div(k, far))

    def slots_of(k, weighted):
        first, second = pair(k)
        parts = []
        for j, (d, cr) in enumerate(((first, 0), (first, 1), (second, 0), (second, 1))):
            block = info[d, cr]
            rank = block[1:2, :group]
            row = lax.broadcasted_iota(jnp.int32, (4 * CAP, group), 0).astype(F32)
            hit = row == rank + float(CAP * j)
            parts.append(jnp.where(hit, block[0:1, :group] if weighted else 1.0, 0.0))
        return jnp.concatenate(parts, axis=1).astype(BF16)

    def select(k, last):
        first, second = pair(k)
        placing = slots_of(k, False)
        for h in range(2):
            block = jnp.concatenate(
                [tok[first, 0, h], tok[first, 1, h], tok[second, 0, h], tok[second, 1, h]], axis=0
            )
            xr[k - 1, me_s, h] = jnp.dot(placing, block, preferred_element_type=F32).astype(BF16)
        for o in range(1, n_seq):
            rows_copy(k, o).start()

    def gate_up(k):
        for o in range(1, n_seq):
            rows_copy(k, o, True).wait_recv()
        tile = min(hid, 256)
        for n in range(hid // tile):
            sums = []
            for g in range(2):
                total = None
                for s in range(n_seq):
                    part = None
                    for h in range(2):
                        at = s * share + h * half
                        term = lax.dot_general(
                            xr[k - 1, s, h], wgu[g, n * tile:(n + 1) * tile, at:at + half],
                            (((1,), (1,)), ((), ())), preferred_element_type=F32,
                        )
                        part = term if part is None else part + term
                    part = part.astype(BF16).astype(F32)
                    total = part if total is None else total + part
                sums.append(total)
            value = sums[0] / (1.0 + jnp.exp(-sums[0])) * sums[1]
            hb[k - 1, me_s, :, n * tile:(n + 1) * tile] = value.astype(BF16)
        for o in range(1, n_seq):
            hidden_copy(k, o).start()

    def down(k):
        for o in range(1, n_seq):
            hidden_copy(k, o, True).wait_recv()
        first, second = pair(k)
        mixing = slots_of(k, True).astype(F32).T.astype(BF16)
        for h in range(2):
            value = None
            for s in range(n_seq):
                term = jnp.dot(
                    hb[k - 1, s], wdn[s * hid:(s + 1) * hid, h * half:(h + 1) * half],
                    preferred_element_type=F32,
                )
                value = term if value is None else value + term
            mixed = jnp.dot(mixing, value.astype(BF16), preferred_element_type=F32).astype(BF16)
            mine[first, h] = mixed[:group]
            pout[first, h] = mixed[group:2 * group]
            mine[second, h] = mixed[2 * group:3 * group]
            pout[second, h] = mixed[3 * group:]
            partial_copy(first, h).start()
            partial_copy(second, h).start()

    for d, cr in others:
        info_copy(d, cr).wait_recv()
    for h in range(2):
        twin_copy(0, h).wait_recv()

    def arrive(way, k, h, forward):
        gather_copy(way, k, h).wait_recv()
        if forward is not None:
            @pl.when(forward)
            def _():
                gather_copy(way, k + 1, h).start()
        twin_copy(chips - k if way == 0 else k, h).start()

    def gather_step(k, carry):
        arrive(0, k, 0, k < far)
        arrive(1, k, 1, k < far)

        @pl.when(k == 3)
        def _():
            load_gu.wait()

        @pl.when(k >= 3)
        def _():
            gate_up(k - 2)

        arrive(0, k, 1, k < far - 1)
        arrive(1, k, 0, k < far - 1)
        for h in range(2):
            twin_copy(k, h).wait_recv()
            twin_copy(chips - k, h).wait_recv()
        select(k, False)
        return carry

    lax.fori_loop(1, far, gather_step, 0)
    if far <= 3:
        load_gu.wait()
    arrive(0, far, 0, None)
    arrive(1, far, 1, None)
    for h in range(2):
        twin_copy(far, h).wait_recv()
    select(far, True)
    load_dn.wait()

    def up_step(k, carry):
        gate_up(k)
        return carry

    def down_step(k, carry):
        down(k)
        return carry

    lax.fori_loop(max(1, far - 2), far, up_step, 0)
    lax.fori_loop(1, far, down_step, 0)
    gate_up(far)
    down(far)

    for k in range(far, 0, -1):
        for way, h in ((0, 1), (1, 0), (0, 0), (1, 1)):
            if k == far and h != way:
                continue
            d = k if way == 0 else chips - k
            partial_copy(d, h).wait_recv()
            value = mine[d, h].astype(F32) + dd[d, h].astype(F32)
            if k + 1 < far or (k + 1 == far and h == way):
                sum_copy(way, k + 1, h).wait_recv()
                value = value + (rr if way == 0 else ll)[k, h].astype(F32)
            (sr if way == 0 else sl)[k - 1, h] = value.astype(BF16)
            sum_copy(way, k, h).start()
    for h in range(2):
        partial_copy(0, h).wait_recv()
        value = mine[0, h].astype(F32) + dd[0, h].astype(F32)
        sum_copy(0, 1, h).wait_recv()
        sum_copy(1, 1, h).wait_recv()
        value = value + rr[0, h].astype(F32) + ll[0, h].astype(F32)
        out_ref[:, h * half:(h + 1) * half] = value.astype(BF16)

    for d, cr in others:
        info_copy(d, cr).wait_send()
    for k in range(1, far + 1):
        for way in range(2):
            for h in range(2):
                if k < far or h == way:
                    gather_copy(way, k, h).wait_send()
                    sum_copy(way, k, h).wait_send()
        for o in range(1, n_seq):
            rows_copy(k, o).wait_send()
            hidden_copy(k, o).wait_send()
    for d in range(chips):
        for h in range(2):
            twin_copy(d, h).wait_send()
            partial_copy(d, h).wait_send()


def body(n_seq, n_expert, tokens, expert_ids, route_weights, capacity, expert_gate_up, expert_down):
    group, share = tokens.shape
    half = share // 2
    hid, width = expert_gate_up.shape[2:]
    units = expert_down.shape[1]
    chips = n_expert // 2
    far = chips // 2
    hit = expert_ids[None, :, :] == jnp.arange(n_expert, dtype=jnp.int32)[:, None, None]
    weight = jnp.sum(jnp.where(hit, route_weights[None], 0.0), axis=2)
    chosen = jnp.any(hit, axis=2)
    earlier = jnp.arange(group)[:, None] < jnp.arange(group)[None, :]
    rank = jnp.dot(chosen.astype(BF16), earlier.astype(BF16), preferred_element_type=F32)
    keep = jnp.logical_and(chosen, rank < capacity.astype(F32)[:, None])
    table = jnp.stack([jnp.where(keep, weight, 0.0), jnp.where(keep, rank, -10000.0)], axis=1)
    table = jnp.pad(table, ((0, 0), (0, 6), (0, -group % 128)))
    blocks = tokens.reshape(group, 2, half).transpose(1, 0, 2)
    sem = pltpu.SemaphoreType.DMA
    rows = 4 * CAP
    block = (group, half)
    return pl.pallas_call(
        functools.partial(kernel, n_seq, n_expert),
        out_shape=jax.ShapeDtypeStruct((group, share), BF16),
        in_specs=[
            pl.BlockSpec(memory_space=pltpu.VMEM),
            pl.BlockSpec(memory_space=pl.ANY),
            pl.BlockSpec(memory_space=pl.ANY),
            pl.BlockSpec(memory_space=pl.ANY),
        ],
        out_specs=pl.BlockSpec(memory_space=pltpu.VMEM),
        scratch_shapes=[
            pltpu.VMEM((2, hid, width), BF16),
            pltpu.VMEM((units, share), BF16),
            pltpu.VMEM((chips, 2, 2) + block, BF16),
            pltpu.VMEM((chips, 2, 8, table.shape[2]), F32),
            pltpu.VMEM((far, n_seq, 2, rows, half), BF16),
            pltpu.VMEM((far, n_seq, rows, hid), BF16),
            pltpu.VMEM((chips, 2) + block, BF16),
            pltpu.VMEM((chips, 2) + block, BF16),
            pltpu.VMEM((chips, 2) + block, BF16),
            pltpu.VMEM((far, 2) + block, BF16),
            pltpu.VMEM((far, 2) + block, BF16),
            pltpu.VMEM((far, 2) + block, BF16),
            pltpu.VMEM((far, 2) + block, BF16),
            sem((4,)),
            sem((chips, 2)), sem((chips, 2)),
            sem((2, far, 2)), sem((2, far, 2)),
            sem((chips, 2)), sem((chips, 2)),
            sem((far, max(1, n_seq - 1))), sem((far, max(1, n_seq - 1))),
            sem((far, max(1, n_seq - 1))), sem((far, max(1, n_seq - 1))),
            sem((chips, 2)), sem((chips, 2)),
            sem((2, far, 2)), sem((2, far, 2)),
        ],
        compiler_params=pltpu.CompilerParams(
            collective_id=0, has_side_effects=True, vmem_limit_bytes=60 * 1024 * 1024
        ),
    )(table, blocks, expert_gate_up[0], expert_down[0])


def solution(mesh):
    in_specs = (
        P("expert", "seq"),
        P("expert", None),
        P("expert", None),
        P(),
        P("expert", None, "seq", None),
        P("expert", None, "seq"),
    )
    return jax.shard_map(
        functools.partial(body, mesh.shape["seq"], mesh.shape["expert"]),
        mesh=mesh, in_specs=in_specs, out_specs=P("expert", "seq"), check_vma=False,
    )
```

time: 198 us -> 106 us (0.54)
  blocking collectives: 105 us -> 0 us
  Pallas kernels: 0 us -> 99.1 us
  local copies, waits for them, and re-layouts: 47.2 us -> 3.46 us
  matrix products: 17.8 us -> 0.07 us
  between operations: 13.5 us -> 0.01 us
  waiting for transfers between devices: 7.89 us -> 0 us
  other arithmetic: 4.79 us -> 2.81 us
    pallas_call x0 -> x1, Pallas kernels: none -> 99.1 us  [body(): pl.pallas_call(functools.partial(kernel, n_seq, n_expert), out_shape=jax....]
    all_to_all x2 -> x0, blocking collectives: 98.2 us -> none  [the longest x1 49.9 us: body(): lax.all_to_all(buffer.reshape(expert_count, CAP, share), 'expert', split_...]
    another operation x1 -> x0, local copies, waits for them, and re-layouts: 32.1 us -> none  [body(): column_blocks = weights.reshape(2, hidden_share, blocks, share)]
    dot_general x4 -> x1, matrix products: 17.8 us -> 0.07 us  [body(): jnp.dot(chosen.astype(BF16), earlier.astype(BF16), preferred_element_type...]
    reshape x5 -> x1, local copies, waits for them, and re-layouts: 12.8 us -> 1.73 us  [body(): blocks = tokens.reshape(group, 2, half).transpose(1, 0, 2)]
    all_gather x1 -> x0, waiting for transfers between devices: 7.88 us -> none  [body(): piece = lax.all_gather(rows, 'seq', axis=1, tiled=True)]
    all_gather x1 -> x0, blocking collectives: 7.14 us -> none  [body(): lax.all_gather(hidden, 'seq', axis=1, tiled=True)]
    reduce_sum x3 -> x1, other arithmetic: 3.06 us -> 0.73 us  [body(): weight = jnp.sum(jnp.where(hit, route_weights[None], 0.0), axis=2)]
  transfers between devices with their start and end apart: 1 -> 0, of which waited for: 1 -> 0; matrix products, arithmetic and copies ran while one was open for 16% -> 0% of each run, Pallas kernels for 0% -> 0%
where the time goes in v1:
time: 106 us; the launch traced here: 105 us
  Pallas kernels  99.1 us (93%)
  local copies, waits for them, and re-layouts  3.46 us (3%)
  other arithmetic  2.81 us (3%)
    pallas_call x1, Pallas kernels, body(): pl.pallas_call(functools.partial(kernel, n_seq, n_expert), out_shape=jax....  99.1 us

profile of v1, /device:TPU:0, one launch (start us, length us, event | category | flops | bytes accessed | tf_op | source)
XLA Modules:
  0.0 105.5 jit_solution(9765231549849256916)
XLA Ops:
  0.0 0.7 convert_element_type.3
  0.7 0.7 fusion
  1.4 0.7 select_reduce_fusion
  2.1 0.1 fusion.3
  2.2 0.7 select_maximum_fusion.info_ref
  2.9 1.7 %copy.18 = bf16[6,2,8,1792]{3,2,0,1:T(8,128)(2,1)} copy(bf16[6,2,8,1792]{3,2,1,0:T(8,128)(2,1)} %bitcast.17) | data formatting | bytes 688128 | tf_op jit(solution)/shard_map/reshape | solution.py:295
  4.6 99.1 %shard_map.64 = bf16[48,3584]{1,0:T(8,128)(2,1)} custom-call(f32[16,8,128]{2,1,0:T(8,128)} %select_maximum_fusion.info_ref, bf16[2,48,1792]{2,1,0:T(8,128)(2,1)} %bitcast.16, bf16[2,512,7168]{2,1,0:T(8,128)(2,1)} %bitcast.14, bf16[1024,3584]{1,0:T(8,128)(2,1)} %bitcast.15), custom_call_target="tpu_custom_call" | custom-call | tf_op jit(solution)/shard_map/pallas_call | solution.py:299
  103.7 1.7 %copy.20 = bf16[48,3584]{1,0:T(8,128)(2,1)} copy(bf16[48,3584]{1,0:T(8,128)(2,1)} %shard_map.64) | data formatting | bytes 688128

commit v2 on v1

v2 whole, which is shorter than its diff:
```python
import functools

import jax
import jax.numpy as jnp
from jax import lax
from jax.experimental import pallas as pl
from jax.experimental.pallas import tpu as pltpu
from jax.sharding import PartitionSpec as P

CAP = 12
MESH = pl.DeviceIdType.MESH
F32 = jnp.float32
BF16 = jnp.bfloat16


def kernel(
    n_seq, n_expert, ids_ref, weight_ref, cap_ref, tokens_ref, gate_up_ref, down_ref, out_ref,
    wgu, wdn, tok, table, info, xr, acc, hb, mine, pout, dd, sr, sl, rr, ll,
    local_sem, info_s, info_r, ag_s, ag_r, tw_s, tw_r, x_s, x_r, h_s, h_r, p_s, p_r, rs_s, rs_r,
):
    chips = n_expert // 2
    far = chips // 2
    group, half = tok.shape[3], tok.shape[4]
    share = 2 * half
    hid = wgu.shape[1]
    rows = xr.shape[3]
    small = -(-2 * CAP // 16) * 16
    aligned = half % 128 == 0
    me_e = lax.axis_index("expert")
    me_s = lax.axis_index("seq")
    core = lax.rem(me_e, 2)
    chip = lax.div(me_e, 2)
    odd = lax.rem(chip, 2)
    pos = (1 - odd) * lax.div(chip, 2) + odd * (chips - 1 - lax.div(chip, 2))

    def device_at(offset, same_core):
        at = lax.rem(pos + offset + 2 * chips, chips)
        back = lax.div(at, far)
        there = (1 - back) * 2 * at + back * (2 * (chips - 1 - at) + 1)
        return there * 2 + (core if same_core else 1 - core)

    right, left, twin = device_at(1, True), device_at(-1, True), device_at(0, False)

    def remote(src, dst, send, recv, device):
        return pltpu.make_async_remote_copy(
            src_ref=src, dst_ref=dst, send_sem=send, recv_sem=recv,
            device_id=device, device_id_type=MESH,
        )

    def info_copy(d, cr):
        to = device_at(-d, cr == 0)
        return remote(table.at[to], info.at[d, cr], info_s.at[d, cr], info_r.at[d, cr], {"expert": to})

    def gather_copy(way, k, h):
        src = lax.rem(chips - k + 1, chips) if way == 0 else k - 1
        dst = chips - k if way == 0 else k
        return remote(
            tok.at[src, 0, h], tok.at[dst, 0, h], ag_s.at[way, k - 1, h], ag_r.at[way, k - 1, h],
            {"expert": right if way == 0 else left},
        )

    def twin_copy(d, h):
        return remote(tok.at[d, 0, h], tok.at[d, 1, h], tw_s.at[d, h], tw_r.at[d, h], {"expert": twin})

    def rows_copy(k, h, o, single, receive=False):
        slot = lax.rem(me_s - o + n_seq, n_seq) if receive else me_s
        span = xr.at[k, slot, h, pl.ds(0, small)] if single else xr.at[k, slot, h]
        return remote(
            span, span, x_s.at[k, h, o - 1], x_r.at[k, h, o - 1], {"seq": lax.rem(me_s + o, n_seq)}
        )

    def hidden_copy(k, o, receive=False):
        slot = lax.rem(me_s - o + n_seq, n_seq) if receive else me_s
        return remote(
            hb.at[k, slot], hb.at[k, slot], h_s.at[k, o - 1], h_r.at[k, o - 1],
            {"seq": lax.rem(me_s + o, n_seq)},
        )

    def partial_copy(d, h):
        return remote(pout.at[d, h], dd.at[d, h], p_s.at[d, h], p_r.at[d, h], {"expert": twin})

    def sum_copy(way, k, h):
        src, dst = (sr, rr) if way == 0 else (sl, ll)
        return remote(
            src.at[k - 1, h], dst.at[k - 1, h], rs_s.at[way, k - 1, h], rs_r.at[way, k - 1, h],
            {"expert": right if way == 0 else left},
        )

    if aligned:
        load_tokens = [
            pltpu.make_async_copy(
                tokens_ref.at[:, pl.ds(h * half, half)], tok.at[0, 0, h], local_sem.at[h]
            )
            for h in range(2)
        ]
    else:
        load_tokens = [pltpu.make_async_copy(tokens_ref, tok.at[0, 0], local_sem.at[0])]
    load_gu = pltpu.make_async_copy(gate_up_ref, wgu, local_sem.at[2])
    load_dn = pltpu.make_async_copy(down_ref, wdn, local_sem.at[3])
    for load in load_tokens:
        load.start()
    load_gu.start()
    load_dn.start()

    barrier = pltpu.get_barrier_semaphore()
    for o in range(1, n_expert):
        pl.semaphore_signal(
            barrier, inc=1, device_id={"expert": lax.rem(me_e + o, n_expert)}, device_id_type=MESH
        )
    for o in range(1, n_seq):
        pl.semaphore_signal(
            barrier, inc=1, device_id={"seq": lax.rem(me_s + o, n_seq)}, device_id_type=MESH
        )
    expert_at = lax.broadcasted_iota(jnp.int32, (n_expert, group), 0)
    weight = jnp.zeros((n_expert, group), F32)
    chosen = jnp.zeros((n_expert, group), F32)
    for c in range(ids_ref.shape[0]):
        hit = expert_at == ids_ref[c:c + 1, :]
        weight = weight + jnp.where(hit, weight_ref[c:c + 1, :], 0.0)
        chosen = chosen + jnp.where(hit, 1.0, 0.0)
    before = lax.broadcasted_iota(jnp.int32, (group, group), 0)
    after = lax.broadcasted_iota(jnp.int32, (group, group), 1)
    earlier = jnp.where(before < after, 1.0, 0.0).astype(BF16)
    rank = jnp.dot(chosen.astype(BF16), earlier, preferred_element_type=F32)
    limit = jnp.zeros((n_expert, group), jnp.int32)
    for e in range(n_expert):
        limit = jnp.where(expert_at == e, cap_ref[e], limit)
    keep = jnp.logical_and(chosen > 0.5, rank < limit.astype(F32))
    weight = jnp.where(keep, weight, 0.0)
    rank = jnp.where(keep, rank, -10000.0)
    for e in range(n_expert):
        table[e, 0:1, :group] = weight[e:e + 1]
        table[e, 1:2, :group] = rank[e:e + 1]
    info[0, 0] = table[me_e]
    for k in (0, far):
        for s in range(n_seq):
            for h in range(2):
                xr[k, s, h, small:] = jnp.zeros((rows - small, half), BF16)
    for load in load_tokens:
        load.wait()
    pl.semaphore_wait(barrier, n_expert - 1 + n_seq - 1)

    others = [(d, cr) for d in range(chips) for cr in range(2) if d or cr]
    for way, h in ((0, 0), (1, 0), (0, 1), (1, 1)):
        gather_copy(way, 1, h).start()
    for h in range(2):
        twin_copy(0, h).start()
    for d, cr in others:
        info_copy(d, cr).start()

    def distances(k, single):
        return (k,) if single else (k, chips - k)

    def slots_of(k, single, weighted, height):
        parts = []
        for d in distances(k, single):
            for cr in range(2):
                block = info[d, cr]
                row = lax.broadcasted_iota(jnp.int32, (height, group), 0).astype(F32)
                hit = row == block[1:2, :group] + float(CAP * len(parts))
                parts.append(jnp.where(hit, block[0:1, :group] if weighted else 1.0, 0.0))
        return jnp.concatenate(parts, axis=1)

    def select(k, h, single):
        height = small if single else rows
        placing = slots_of(k, single, False, height).astype(BF16)
        for d in distances(k, single):
            twin_copy(d, h).wait_recv()
        block = jnp.concatenate([tok[d, cr, h] for d in distances(k, single) for cr in range(2)], axis=0)
        xr[k, me_s, h, :height] = jnp.dot(placing, block, preferred_element_type=F32).astype(BF16)
        for o in range(1, n_seq):
            rows_copy(k, h, o, single).start()

    def take_info(k, single):
        for d in distances(k, single):
            info_copy(d, 1).wait_recv()
            if not (single and isinstance(d, int) and d == 0):
                info_copy(d, 0).wait_recv()

    def block_sum(k, s, dynamic):
        total = None
        for h in range(2):
            at = s * share + h * half
            columns = pl.ds(pl.multiple_of(at, 128), half) if dynamic else slice(at, at + half)
            term = [
                lax.dot_general(
                    xr[k, s, h], wgu[g, :, columns], (((1,), (1,)), ((), ())),
                    preferred_element_type=F32,
                )
                for g in range(2)
            ]
            total = term if total is None else [a + b for a, b in zip(total, term)]
        return [a.astype(BF16).astype(F32) for a in total]

    def gate_own(k):
        if aligned:
            own = block_sum(k, me_s, True)
            for g in range(2):
                acc[k, g] = own[g]

    def gate_rest(k, single):
        for o in range(1, n_seq):
            for h in range(2):
                rows_copy(k, h, o, single, True).wait_recv()
        if aligned:
            total = [acc[k, g] for g in range(2)]
            for o in range(1, n_seq):
                more = block_sum(k, lax.rem(me_s - o + n_seq, n_seq), True)
                total = [a + b for a, b in zip(total, more)]
        else:
            total = block_sum(k, 0, False)
            for s in range(1, n_seq):
                total = [a + b for a, b in zip(total, block_sum(k, s, False))]
        value = total[0] / (1.0 + jnp.exp(-total[0])) * total[1]
        hb[k, me_s] = value.astype(BF16)
        for o in range(1, n_seq):
            hidden_copy(k, o).start()

    def down(k, single):
        for o in range(1, n_seq):
            hidden_copy(k, o, True).wait_recv()
        mixing = slots_of(k, single, True, rows).T.astype(BF16)
        for h in range(2):
            value = None
            for s in range(n_seq):
                term = jnp.dot(
                    hb[k, s], wdn[s * hid:(s + 1) * hid, h * half:(h + 1) * half],
                    preferred_element_type=F32,
                )
                value = term if value is None else value + term
            mixed = jnp.dot(mixing, value.astype(BF16), preferred_element_type=F32).astype(BF16)
            for j, d in enumerate(distances(k, single)):
                mine[d, h] = mixed[2 * j * group:(2 * j + 1) * group]
                pout[d, h] = mixed[(2 * j + 1) * group:(2 * j + 2) * group]
                partial_copy(d, h).start()

    def arrive(way, k, h, forward):
        gather_copy(way, k, h).wait_recv()
        if forward is not None:
            @pl.when(forward)
            def _():
                gather_copy(way, k + 1, h).start()
        twin_copy(chips - k if way == 0 else k, h).start()

    take_info(0, True)
    for h in range(2):
        select(0, h, True)

    def gather_step(k, carry):
        arrive(0, k, 0, k < far)
        arrive(1, k, 0, k < far - 1)
        take_info(k, False)
        select(k, 0, False)

        @pl.when(k == 2)
        def _():
            load_gu.wait()
            gate_own(0)

        @pl.when(k >= 3)
        def _():
            gate_rest(k - 2, False)

        arrive(0, k, 1, k < far - 1)
        arrive(1, k, 1, k < far)
        select(k, 1, False)

        @pl.when(k >= 2)
        def _():
            gate_own(k - 1)

        @pl.when(k == 2)
        def _():
            gate_rest(0, True)

        return carry

    lax.fori_loop(1, far, gather_step, 0)
    gate_own(far - 1)
    arrive(0, far, 0, None)
    arrive(1, far, 1, None)
    take_info(far, True)
    for h in range(2):
        select(far, h, True)
    gate_own(far)
    load_dn.wait()

    def rest_step(k, carry):
        gate_rest(k, False)
        return carry

    lax.fori_loop(far - 2, far, rest_step, 0)
    gate_rest(far, True)
    down(far - 1, False)
    down(far, True)

    def reduce_step(k, first, second):
        for way, h in ((0, 1), (1, 0), (0, 0), (1, 1)):
            if first and h != way:
                continue
            d = k if way == 0 else chips - k
            partial_copy(d, h).wait_recv()
            value = mine[d, h].astype(F32) + dd[d, h].astype(F32)
            if not first and not (second and h != way):
                sum_copy(way, k + 1, h).wait_recv()
                value = value + (rr if way == 0 else ll)[k, h].astype(F32)
            (sr if way == 0 else sl)[k - 1, h] = value.astype(BF16)
            sum_copy(way, k, h).start()

    reduce_step(far, True, False)
    reduce_step(far - 1, False, True)

    def tail_step(i, carry):
        k = far - 2 - i
        down(k, False)
        reduce_step(k, False, False)
        return carry

    lax.fori_loop(0, far - 2, tail_step, 0)
    down(0, True)
    for h in range(2):
        partial_copy(0, h).wait_recv()
        value = mine[0, h].astype(F32) + dd[0, h].astype(F32)
        sum_copy(0, 1, h).wait_recv()
        sum_copy(1, 1, h).wait_recv()
        value = value + rr[0, h].astype(F32) + ll[0, h].astype(F32)
        out_ref[:, h * half:(h + 1) * half] = value.astype(BF16)

    for d, cr in others:
        info_copy(d, cr).wait_send()
    for k in range(1, far + 1):
        for way in range(2):
            for h in range(2):
                if k < far or h == way:
                    gather_copy(way, k, h).wait_send()
                    sum_copy(way, k, h).wait_send()
    for k in range(far + 1):
        for o in range(1, n_seq):
            hidden_copy(k, o).wait_send()
            for h in range(2):
                rows_copy(k, h, o, k in (0, far)).wait_send()
    for d in range(chips):
        for h in range(2):
            twin_copy(d, h).wait_send()
            partial_copy(d, h).wait_send()


def body(n_seq, n_expert, tokens, expert_ids, route_weights, capacity, expert_gate_up, expert_down):
    group, share = tokens.shape
    half = share // 2
    hid, width = expert_gate_up.shape[2:]
    units = expert_down.shape[1]
    chips = n_expert // 2
    far = chips // 2
    lanes = -(-group // 128) * 128
    aligned = half % 128 == 0
    blocks = tokens if aligned else tokens.reshape(group, 2, half).transpose(1, 0, 2)
    sem = pltpu.SemaphoreType.DMA
    rows = 4 * CAP
    block = (group, half)
    return pl.pallas_call(
        functools.partial(kernel, n_seq, n_expert),
        out_shape=jax.ShapeDtypeStruct((group, share), BF16),
        in_specs=[
            pl.BlockSpec(memory_space=pltpu.VMEM),
            pl.BlockSpec(memory_space=pltpu.VMEM),
            pl.BlockSpec(memory_space=pltpu.SMEM),
            pl.BlockSpec(memory_space=pl.ANY),
            pl.BlockSpec(memory_space=pl.ANY),
            pl.BlockSpec(memory_space=pl.ANY),
        ],
        out_specs=pl.BlockSpec(memory_space=pltpu.VMEM),
        scratch_shapes=[
            pltpu.VMEM((2, hid, width), BF16),
            pltpu.VMEM((units, share), BF16),
            pltpu.VMEM((chips, 2, 2) + block, BF16),
            pltpu.VMEM((n_expert, 8, lanes), F32),
            pltpu.VMEM((chips, 2, 8, lanes), F32),
            pltpu.VMEM((far + 1, n_seq, 2, rows, half), BF16),
            pltpu.VMEM((far + 1, 2, rows, hid), F32),
            pltpu.VMEM((far + 1, n_seq, rows, hid), BF16),
            pltpu.VMEM((chips, 2) + block, BF16),
            pltpu.VMEM((chips, 2) + block, BF16),
            pltpu.VMEM((chips, 2) + block, BF16),
            pltpu.VMEM((far, 2) + block, BF16),
            pltpu.VMEM((far, 2) + block, BF16),
            pltpu.VMEM((far, 2) + block, BF16),
            pltpu.VMEM((far, 2) + block, BF16),
            sem((4,)),
            sem((chips, 2)), sem((chips, 2)),
            sem((2, far, 2)), sem((2, far, 2)),
            sem((chips, 2)), sem((chips, 2)),
            sem((far + 1, 2, max(1, n_seq - 1))), sem((far + 1, 2, max(1, n_seq - 1))),
            sem((far + 1, max(1, n_seq - 1))), sem((far + 1, max(1, n_seq - 1))),
            sem((chips, 2)), sem((chips, 2)),
            sem((2, far, 2)), sem((2, far, 2)),
        ],
        compiler_params=pltpu.CompilerParams(
            collective_id=0, has_side_effects=True, vmem_limit_bytes=60 * 1024 * 1024
        ),
    )(expert_ids.T, route_weights.T, capacity, blocks, expert_gate_up[0], expert_down[0])


def solution(mesh):
    in_specs = (
        P("expert", "seq"),
        P("expert", None),
        P("expert", None),
        P(),
        P("expert", None, "seq", None),
        P("expert", None, "seq"),
    )
    return jax.shard_map(
        functools.partial(body, mesh.shape["seq"], mesh.shape["expert"]),
        mesh=mesh, in_specs=in_specs, out_specs=P("expert", "seq"), check_vma=False,
    )
```

time: 106 us -> 92.4 us (0.87)
  Pallas kernels: 99.1 us -> 90.5 us
  other arithmetic: 2.81 us -> 0 us
  local copies, waits for them, and re-layouts: 3.46 us -> 1.73 us
    pallas_call x1, Pallas kernels: 99.1 us -> 90.5 us  [body(): pl.pallas_call(functools.partial(kernel, n_seq, n_expert), out_shape=jax....]
    reshape x1 -> x0, local copies, waits for them, and re-layouts: 1.73 us -> none  [body(): blocks = tokens.reshape(group, 2, half).transpose(1, 0, 2)]
where the time goes in v2:
time: 92.4 us; the launch traced here: 92.2 us
  Pallas kernels  90.5 us (98%)
  local copies, waits for them, and re-layouts  1.73 us (2%)
    pallas_call x1, Pallas kernels, body(): pl.pallas_call(functools.partial(kernel, n_seq, n_expert), out_shape=jax....  90.5 us

profile of v2, /device:TPU:0, one launch (start us, length us, event | category | flops | bytes accessed | tf_op | source)
XLA Modules:
  0.0 92.2 jit_solution(6640923569245996612)
XLA Ops:
  0.0 90.5 %shard_map.64 = bf16[48,3584]{1,0:T(8,128)(2,1)} custom-call(s32[8,48]{1,0:T(8,128)} %bitcast.6, f32[8,48]{1,0:T(8,128)} %bitcast.7, s32[16]{0:T(128)} %cap_ref.1, bf16[48,3584]{1,0:T(8,128)(2,1)} %tokens_ref.1, bf16[2,512,7168]{2,1,0:T(8,128)(2,1)} %bitcast.4, bf16[1024,3584]{1,0:T(8,128)(2,1)} %bitcast.5), custom_call_target="tpu_custom_call" | custom-call | tf_op jit(solution)/shard_map/pallas_call | solution.py:361
  90.5 1.7 %copy.8 = bf16[48,3584]{1,0:T(8,128)(2,1)} copy(bf16[48,3584]{1,0:T(8,128)(2,1)} %shard_map.64) | data formatting | bytes 688128

commit v3 on v2

--- a/solution.py
+++ b/solution.py
@@ -141,11 +141,15 @@
     pl.semaphore_wait(barrier, n_expert - 1 + n_seq - 1)
 
     others = [(d, cr) for d in range(chips) for cr in range(2) if d or cr]
+    others.sort(key=lambda at: min(at[0], chips - at[0]))
+    near = [at for at in others if min(at[0], chips - at[0]) <= 1]
+    for d, cr in near:
+        info_copy(d, cr).start()
     for way, h in ((0, 0), (1, 0), (0, 1), (1, 1)):
         gather_copy(way, 1, h).start()
     for h in range(2):
         twin_copy(0, h).start()
-    for d, cr in others:
+    for d, cr in others[len(near):]:
         info_copy(d, cr).start()
 
     def distances(k, single):
@@ -269,10 +273,6 @@
         def _():
             gate_own(k - 1)
 
-        @pl.when(k == 2)
-        def _():
-            gate_rest(0, True)
-
         return carry
 
     lax.fori_loop(1, far, gather_step, 0)
@@ -294,29 +294,32 @@
     down(far - 1, False)
     down(far, True)
 
-    def reduce_step(k, first, second):
-        for way, h in ((0, 1), (1, 0), (0, 0), (1, 1)):
-            if first and h != way:
-                continue
+    def reduce_step(k, fresh, held):
+        for way, h in [(0, 1), (1, 0)] * fresh + [(0, 0), (1, 1)] * held:
             d = k if way == 0 else chips - k
             partial_copy(d, h).wait_recv()
             value = mine[d, h].astype(F32) + dd[d, h].astype(F32)
-            if not first and not (second and h != way):
+            starts = isinstance(k, int) and (k == far or (k == far - 1 and h != way))
+            if not starts:
                 sum_copy(way, k + 1, h).wait_recv()
                 value = value + (rr if way == 0 else ll)[k, h].astype(F32)
             (sr if way == 0 else sl)[k - 1, h] = value.astype(BF16)
             sum_copy(way, k, h).start()
 
-    reduce_step(far, True, False)
+    reduce_step(far, False, True)
+    reduce_step(far - 1, True, False)
+    down(far - 2, False)
     reduce_step(far - 1, False, True)
 
     def tail_step(i, carry):
         k = far - 2 - i
-        down(k, False)
-        reduce_step(k, False, False)
+        down(k - 1, False)
+        reduce_step(k, True, True)
         return carry
 
-    lax.fori_loop(0, far - 2, tail_step, 0)
+    lax.fori_loop(0, far - 3, tail_step, 0)
+    gate_rest(0, True)
+    reduce_step(1, True, True)
     down(0, True)
     for h in range(2):
         partial_copy(0, h).wait_recv()

time: 92.4 us -> 90.1 us (0.975)
  Pallas kernels: 90.5 us -> 88.1 us
    pallas_call x1, Pallas kernels: 90.5 us -> 88.1 us  [body(): pl.pallas_call(functools.partial(kernel, n_seq, n_expert), out_shape=jax....]
where the time goes in v3:
time: 90.1 us; the launch traced here: 89.9 us
  Pallas kernels  88.1 us (98%)
  local copies, waits for them, and re-layouts  1.73 us (2%)
    pallas_call x1, Pallas kernels, body(): pl.pallas_call(functools.partial(kernel, n_seq, n_expert), out_shape=jax....  88.1 us

profile of v3, /device:TPU:0, one launch (start us, length us, event | category | flops | bytes accessed | tf_op | source)
XLA Modules:
  0.0 89.9 jit_solution(2665206199750900004)
XLA Ops:
  0.0 88.1 %shard_map.64 = bf16[48,3584]{1,0:T(8,128)(2,1)} custom-call(s32[8,48]{1,0:T(8,128)} %bitcast.6, f32[8,48]{1,0:T(8,128)} %bitcast.7, s32[16]{0:T(128)} %cap_ref.1, bf16[48,3584]{1,0:T(8,128)(2,1)} %tokens_ref.1, bf16[2,512,7168]{2,1,0:T(8,128)(2,1)} %bitcast.4, bf16[1024,3584]{1,0:T(8,128)(2,1)} %bitcast.5), custom_call_target="tpu_custom_call" | custom-call | tf_op jit(solution)/shard_map/pallas_call | solution.py:364
  88.2 1.7 %copy.8 = bf16[48,3584]{1,0:T(8,128)(2,1)} copy(bf16[48,3584]{1,0:T(8,128)(2,1)} %shard_map.64) | data formatting | bytes 688128
